TPU v7x, 32 devices: a whole 2x2x4 slice. The times are simulated.
32 devices in a mesh: pair: 16 (over z, y, x), sector: 2 (over core).
Axes of the slice: x: 2, y: 2, z: 4, core: 2. Of those that a mesh axis runs over, the one named last changes fastest.
Arguments:
- wavefunction: float32 [2, 512, 512], P('sector', 'pair'), may hold values from -6 to 6
- preconditioner: float32 [2, 512, 512], P('sector', 'pair'), may hold values from 0.5 to 4
- left_ops: float32 [48, 2, 512, 512], P('pair', 'sector'), may hold values from -0.25 to 0.25
- right_ops: float32 [48, 2, 512, 512], P('pair', 'sector'), may hold values from -0.02734375 to 0.02734375
- charges: int32 [48], P('pair'), may hold values from 0 to 2
- coupling: int32 [2, 3], P('sector'), may hold values 0 or 1
Outputs:
- new_state: float32 [2, 512, 512], P('sector', 'pair')
- new_image: float32 [2, 512, 512], P('sector', 'pair')
- energies: float32 [2], replicated
All inputs are finite; a program needn't handle non-finite values. No bound on the sum of `coupling` on one device may be relied on, other than what follows from the above.
Results may differ from a plain program's by a relative error of at most 0.0003.
Values sent between devices are 32-bit elements; how exact they have to be, the bound alone decides.
No kernel may reach another device: no remote copies, remote signals or barrier semaphores. Data moves between devices by JAX's collectives and lax.ppermute only.
A program may use at most 64 MiB of HBM per device.

v0:
```python
import math
import jax
import jax.numpy as jnp
from jax import lax
from jax.sharding import PartitionSpec as P

highest = lax.Precision.HIGHEST


def shifted(block, axis, distance):
    devices = range(lax.axis_size(axis))
    route = [((i - distance) % len(devices), i) for i in devices]
    return lax.ppermute(block, axis, route)


def product(first, second):
    return jnp.dot(first, second, precision=highest, preferred_element_type=jnp.float32)


def sigma_apply(vector, left_ops, right_ops, charges, coupling):
    lower_rows = shifted(vector, "sector", 1)
    upper_rows = shifted(vector, "sector", -1)
    gathered = (
        lax.all_gather(lower_rows, "pair", axis=1, tiled=True),
        lax.all_gather(vector, "pair", axis=1, tiled=True),
        lax.all_gather(upper_rows, "pair", axis=1, tiled=True),
    )
    stacked = jnp.concatenate(gathered, axis=0)
    own_block = stacked[1]
    targets = jnp.zeros_like(stacked)
    for which_pair in range(left_ops.shape[0]):
        left_block = left_ops[which_pair, 0]
        right_block = right_ops[which_pair, 0]
        charge_slot = charges[which_pair]
        allowed = lax.dynamic_index_in_dim(coupling[0], charge_slot, 0, keepdims=False).astype(
            jnp.float32
        )
        source_block = lax.dynamic_index_in_dim(stacked, charge_slot, 0, keepdims=False)
        forward = product(product(left_block, own_block), right_block.T)
        backward = product(product(left_block.T, source_block), right_block)
        current = lax.dynamic_index_in_dim(targets, charge_slot, 0, keepdims=False)
        targets = lax.dynamic_update_index_in_dim(
            targets, current + allowed * forward, charge_slot, 0
        )
        targets = targets.at[1].add(allowed * backward)
    from_below = shifted(targets[2], "sector", 1)
    from_above = shifted(targets[0], "sector", -1)
    combined = targets[1] + from_below + from_above
    return lax.psum_scatter(combined[None], "pair", scatter_dimension=1, tiled=True)


def per_device(wavefunction, preconditioner, left_ops, right_ops, charges, coupling):
    first_image = sigma_apply(wavefunction, left_ops, right_ops, charges, coupling)
    norm_sq, correlation = lax.psum(
        (jnp.sum(wavefunction * wavefunction), jnp.sum(wavefunction * first_image)),
        ("pair", "sector"),
    )
    theta = correlation / norm_sq
    inverse = lax.rsqrt(norm_sq)
    vector = wavefunction * inverse
    image = first_image * inverse
    residual = image - theta * vector
    correction = residual / preconditioner
    along, squared = lax.psum(
        (jnp.sum(vector * correction), jnp.sum(correction * correction)), ("pair", "sector")
    )
    orthogonal = correction - along * vector
    length_sq = squared - along * along
    basis = orthogonal * lax.rsqrt(length_sq + 1e-30)
    second_image = sigma_apply(basis, left_ops, right_ops, charges, coupling)
    corner, cross = lax.psum(
        (jnp.sum(basis * second_image), jnp.sum(vector * second_image)), ("pair", "sector")
    )
    half = (theta - corner) / 2.0
    lowest = (theta + corner) / 2.0 - jnp.sqrt(half * half + cross * cross)
    first_weight = corner - lowest
    second_weight = -cross
    size_norm = jnp.sqrt(first_weight * first_weight + second_weight * second_weight + 1e-30)
    entries = (
        lax.axis_size("sector")
        * lax.axis_size("pair")
        * wavefunction.shape[1]
        * wavefunction.shape[2]
    )
    scale = jnp.float32(math.sqrt(entries))
    factor_one = scale * first_weight / size_norm
    factor_two = scale * second_weight / size_norm
    new_state = factor_one * vector + factor_two * basis
    new_image = factor_one * image + factor_two * second_image
    energies = jnp.stack([theta, lowest])
    return (new_state, new_image, energies)


def solution(mesh):
    in_specs = (
        P("sector", "pair", None),
        P("sector", "pair", None),
        P("pair", "sector", None, None),
        P("pair", "sector", None, None),
        P("pair"),
        P("sector", None),
    )
    out_specs = (P("sector", "pair", None), P("sector", "pair", None), P())
    return jax.shard_map(
        per_device, mesh=mesh, in_specs=in_specs, out_specs=out_specs, check_vma=False
    )
```

profile of v0, /device:TPU:12, one launch (start us, length us, event | category | flops | bytes accessed | tf_op | source)
XLA Modules:
  0.0 604.5 jit_solution(9496863320256029471)
XLA Ops:
  21.0 45.0 %all-gather.5.cloned.1.call-done = f32[1,512,512]{2,1,0:T(8,128)} async-done(((f32[1,32,512]{2,1,0:T(8,128)}), f32[1,512,512]{2,1,0:T(8,128)}) %all-gather.5.cloned.1.call-update) | async-done | bytes 1048592 | tf_op jit(solution)/shard_map/all_gather | solution.py:25
  66.0 3.4 fusion.82
  69.4 2.0 broadcast.76.clone
  71.5 4.4 fusion.21
  75.9 2.8 fusion.72
  78.7 2.9 fusion.61
  81.5 41.8 %all-gather.7.cloned.1.call-done = f32[1,512,512]{2,1,0:T(8,128)} async-done(((f32[1,32,512]{2,1,0:T(8,128)}), f32[1,512,512]{2,1,0:T(8,128)}) %all-gather.7.cloned.1.call-update) | async-done | bytes 1048592 | tf_op jit(solution)/shard_map/all_gather | solution.py:24
  126.1 1.9 fusion.63
  128.0 1.9 fusion.74
  130.0 4.5 fusion.23
  135.8 2.8 fusion.18
  138.6 4.2 fusion.25
  144.1 2.9 fusion.14
  152.9 4.3 fusion.39
  157.2 68.8 %reduce-scatter.3.cloned.1.call-done = f32[1,32,512]{2,1,0:T(8,128)} async-done(((f32[1,512,512]{2,1,0:T(8,128)}), f32[1,32,512]{2,1,0:T(8,128)}) %reduce-scatter.3.cloned.1.call-update) | async-done | bytes 65552 | tf_op jit(solution)/shard_map/reduce_scatter | solution.py:49
  227.5 49.3 %all-reduce.2 = (f32[]{:T(128)}, f32[]{:T(128)}) all-reduce(f32[]{:T(128)} %get-tuple-element.80, f32[]{:T(128)} %get-tuple-element.79), channel_id=1, replica_groups=mesh['pair'=16,'sector'=2] {'pair','sector'}, use_global_device_ids=true, to_apply=%region_4.5 | all-reduce | flops 2 | bytes 16 | tf_op jit(solution)/shard_map/psum | solution.py:54
  280.4 38.5 %all-reduce.1 = (f32[]{:T(128)}, f32[]{:T(128)}) all-reduce(f32[]{:T(128)} %get-tuple-element.78, f32[]{:T(128)} %get-tuple-element.77), channel_id=1, replica_groups=mesh['pair'=16,'sector'=2] {'pair','sector'}, use_global_device_ids=true, to_apply=%region_8.9 | all-reduce | flops 2 | bytes 16 | tf_op jit(solution)/shard_map/psum | solution.py:64
  324.6 52.9 %all-gather.9.cloned.1.call-done = f32[1,512,512]{2,1,0:T(8,128)} async-done(((f32[1,32,512]{2,1,0:T(8,128)}), f32[1,512,512]{2,1,0:T(8,128)}) %all-gather.9.cloned.1.call-update) | async-done | bytes 1048592 | tf_op jit(solution)/shard_map/all_gather | solution.py:25
  377.5 4.7 fusion.50
  382.2 2.0 broadcast.76
  384.2 5.7 fusion.10
  389.9 4.5 fusion.48
  394.4 4.7 fusion.46
  399.0 35.6 %all-gather.11.cloned.1.call-done = f32[1,512,512]{2,1,0:T(8,128)} async-done(((f32[1,32,512]{2,1,0:T(8,128)}), f32[1,512,512]{2,1,0:T(8,128)}) %all-gather.11.cloned.1.call-update) | async-done | bytes 1048592 | tf_op jit(solution)/shard_map/all_gather | solution.py:24
  437.4 1.9 fusion.42
  441.3 4.2 fusion.29
  446.7 4.5 fusion.7
  451.2 4.4 fusion.31
  456.9 4.5 fusion.3
  467.4 4.3 fusion.36
  471.7 68.7 %reduce-scatter.5.cloned.1.call-done = f32[1,32,512]{2,1,0:T(8,128)} async-done(((f32[1,512,512]{2,1,0:T(8,128)}), f32[1,32,512]{2,1,0:T(8,128)}) %reduce-scatter.5.cloned.1.call-update) | async-done | bytes 65552 | tf_op jit(solution)/shard_map/reduce_scatter | solution.py:49
  541.9 49.2 %all-reduce = (f32[]{:T(128)}, f32[]{:T(128)}) all-reduce(f32[]{:T(128)} %get-tuple-element.76, f32[]{:T(128)} %get-tuple-element.75), channel_id=1, replica_groups=mesh['pair'=16,'sector'=2] {'pair','sector'}, use_global_device_ids=true, to_apply=%region_13.14 | all-reduce | flops 2 | bytes 16 | tf_op jit(solution)/shard_map/psum | solution.py:71
  (81 shorter events, 40.6 us)
Async XLA Ops:
  7.2 58.8 %all-gather.5.cloned.1.call-start = ((), (), s32[]{:S(2)}) async-start(), calls=%async_computation.2 | async-start | bytes 1114112 | tf_op jit(solution)/shard_map/all_gather | solution.py:25
  7.9 115.4 %all-gather.7.cloned.1.call-start = ((), (), s32[]{:S(2)}) async-start(), calls=%async_computation.3 | async-start | bytes 1114112 | tf_op jit(solution)/shard_map/all_gather | solution.py:24
  7.9 1.5 collective-permute-start
  9.5 0.6 copy-start.14
  10.1 215.9 %reduce-scatter.3.cloned.1.call-start = ((), (), s32[]{:S(2)}) async-start(), calls=%async_computation.4 | async-start | bytes 1114112 | tf_op jit(solution)/shard_map/reduce_scatter | solution.py:49
  69.4 6.5 %copy-start = (f32[3,1,512,512]{3,2,1,0:T(8,128)S(1)}, f32[3,1,512,512]{3,2,1,0:T(8,128)}, u32[]{:S(2)}) copy-start(f32[3,1,512,512]{3,2,1,0:T(8,128)} %param.20) | copy-start | bytes 9437188
  69.4 6.5 %copy-start.3 = (f32[1,512,512]{2,1,0:T(8,128)S(1)}, f32[1,512,512]{2,1,0:T(8,128)}, u32[]{:S(2)}) copy-start(f32[1,512,512]{2,1,0:T(8,128)} %all-gather.5.cloned.1.call-done) | copy-start | bytes 3145732
  123.3 2.7 copy-start.9
  126.1 3.9 copy-start.1
  130.0 5.8 copy-start.8
  138.6 5.5 copy-start.6
  148.7 2.7 collective-permute-start.1
  148.8 4.1 collective-permute-start.2
  151.2 74.9 %copy-start.11 = (f32[1,32,512]{2,1,0:T(8,128)S(1)}, f32[1,32,512]{2,1,0:T(8,128)}, u32[]{:S(2)}) copy-start(f32[1,32,512]{2,1,0:T(8,128)} %param.18) | copy-start | bytes 196612
  151.2 127.7 %copy-start.16 = (f32[1,32,512]{2,1,0:T(8,128)S(1)}, f32[1,32,512]{2,1,0:T(8,128)}, u32[]{:S(2)}) copy-start(f32[1,32,512]{2,1,0:T(8,128)} %param.19) | copy-start | bytes 196612
  157.2 220.3 %all-gather.9.cloned.1.call-start = ((), (), s32[]{:S(2)}) async-start(), calls=%async_computation.5 | async-start | bytes 1114112 | tf_op jit(solution)/shard_map/all_gather | solution.py:25
  322.1 112.5 %all-gather.11.cloned.1.call-start = ((), (), s32[]{:S(2)}) async-start(), calls=%async_computation.6 | async-start | bytes 1114112 | tf_op jit(solution)/shard_map/all_gather | solution.py:24
  322.2 1.5 collective-permute-start.3
  323.7 0.6 copy-start.15
  324.4 216.0 %reduce-scatter.5.cloned.1.call-start = ((), (), s32[]{:S(2)}) async-start(), calls=%async_computation.7 | async-start | bytes 1114112 | tf_op jit(solution)/shard_map/reduce_scatter | solution.py:49
  382.2 7.7 %copy-start.4 = (f32[1,512,512]{2,1,0:T(8,128)S(1)}, f32[1,512,512]{2,1,0:T(8,128)}, u32[]{:S(2)}) copy-start(f32[1,512,512]{2,1,0:T(8,128)} %all-gather.9.cloned.1.call-done) | copy-start | bytes 3145732
  434.6 2.7 copy-start.10
  437.4 3.9 copy-start.2
  441.3 5.5 copy-start.7
  451.2 5.7 copy-start.5
  463.1 2.7 collective-permute-start.4
  463.2 4.1 collective-permute-start.5
  465.6 74.7 %copy-start.12 = (f32[1,32,512]{2,1,0:T(8,128)S(1)}, f32[1,32,512]{2,1,0:T(8,128)}, u32[]{:S(2)}) copy-start(f32[1,32,512]{2,1,0:T(8,128)} %subtract_multiply_fusion) | copy-start | bytes 196612
  465.7 130.1 %copy-start.13 = (f32[1,32,512]{2,1,0:T(8,128)S(1)}, f32[1,32,512]{2,1,0:T(8,128)}, u32[]{:S(2)}) copy-start(f32[1,32,512]{2,1,0:T(8,128)} %reduce-scatter.3.cloned.1.call-done) | copy-start | bytes 196612
Sparse Core Ops, SparseCore 0:
  10.7 55.2 all-gather.4
  69.3 53.9 all-gather.6
  157.3 68.7 reduce-scatter.2
  322.3 55.1 all-gather.8
  380.6 53.9 all-gather.10
  471.8 68.5 reduce-scatter.4
where the time goes:
time: 615 us; the launch traced here: 605 us
  waiting for transfers between devices  320 us (52%)
  blocking collectives  137 us (22%)
  matrix products  84.9 us (14%)
  between operations  30.9 us (5%)
  local copies, waits for them, and re-layouts  22.4 us (4%)
  other arithmetic  7.79 us (1%)
    reduce_scatter x2, waiting for transfers between devices, sigma_apply(): lax.psum_scatter(combined[None], 'pair', scatter_dimension=1, tiled=True)  138 us
    all_gather x2, waiting for transfers between devices, sigma_apply(): lax.all_gather(vector, 'pair', axis=1, tiled=True)  97.9 us
    dot_general x24, matrix products, product(): jnp.dot(first, second, precision=highest, preferred_element_type=jnp.floa...  84.9 us
    all_gather x2, waiting for transfers between devices, sigma_apply(): lax.all_gather(lower_rows, 'pair', axis=1, tiled=True)  77.3 us
    psum x1, blocking collectives, per_device(): lax.psum((jnp.sum(wavefunction * wavefunction), jnp.sum(wavefunction * fi...  49.3 us
    psum x1, blocking collectives, per_device(): lax.psum((jnp.sum(basis * second_image), jnp.sum(vector * second_image)),...  49.2 us
    psum x1, blocking collectives, per_device(): lax.psum((jnp.sum(vector * correction), jnp.sum(correction * correction))...  38.5 us
  transfers between devices with their start and end apart: 12, of which 12 were waited for; matrix products, arithmetic and copies ran while one was open for 7% of the time, Pallas kernels for 0%

commit v1 on v0

--- a/solution.py
+++ b/solution.py
@@ -1,10 +1,43 @@
+import functools
 import math
 import jax
 import jax.numpy as jnp
 from jax import lax
 from jax.sharding import PartitionSpec as P
+from jax.lax import axis_index, axis_size, ppermute
 
 highest = lax.Precision.HIGHEST
+
+
+def prepare_groups(t0, where_dim):
+    work_now = list(t0.shape[1:])
+    work_now[where_dim] *= t0.shape[0]
+    return jnp.moveaxis(t0, 0, where_dim).reshape(work_now)
+
+
+def process_packet(w_in, row_axis):
+    x_now = axis_index(row_axis)
+    current_value = axis_size(row_axis)
+    t_next, k_now = (current_value, x_now)
+    w2, y = (w_in[None], 1)
+    while y < t_next:
+        mat_out = ppermute(
+            w2, axis_name=row_axis, perm=[(hop_no, hop_no ^ y) for hop_no in range(t_next)]
+        )
+        tall = k_now & y == 0
+        ready = jnp.where(tall, w2, mat_out)
+        earlier = jnp.where(tall, mat_out, w2)
+        w2 = jnp.concatenate([ready, earlier])
+        y *= 2
+    return w2
+
+
+def spread_thing(payload, xx, array_dim):
+    x_next = process_packet(payload, xx)
+    return prepare_groups(x_next, array_dim)
+
+
+test_the_heaps = functools.partial(spread_thing, xx="pair", array_dim=1)
 
 
 def shifted(block, axis, distance):
@@ -21,7 +54,7 @@
     lower_rows = shifted(vector, "sector", 1)
     upper_rows = shifted(vector, "sector", -1)
     gathered = (
-        lax.all_gather(lower_rows, "pair", axis=1, tiled=True),
+        test_the_heaps(lower_rows),
         lax.all_gather(vector, "pair", axis=1, tiled=True),
         lax.all_gather(upper_rows, "pair", axis=1, tiled=True),
     )

time: 615 us -> 647 us (1.052)
  other arithmetic: 7.79 us -> 19.6 us
  starting transfers between devices: 1.69 us -> 13.2 us
  matrix products: 84.9 us -> 94.3 us
  local copies, waits for them, and re-layouts: 22.4 us -> 15.5 us
    ppermute x0 -> x8, waiting for transfers between devices: none -> 60.2 us  [process_packet(): ppermute(w2, axis_name=row_axis, perm=[(hop_no, hop_no ^ y) for hop_no in...]
    all_gather x2, waiting for transfers between devices: 97.9 us -> 43.9 us  [sigma_apply(): lax.all_gather(vector, 'pair', axis=1, tiled=True)]
    ppermute x0 -> x8, starting transfers between devices: none -> 11.7 us  [process_packet(): ppermute(w2, axis_name=row_axis, perm=[(hop_no, hop_no ^ y) for hop_no in...]
    dot_general x24, matrix products: 84.9 us -> 94.3 us  [product(): jnp.dot(first, second, precision=highest, preferred_element_type=jnp.floa...]
    concatenate x0 -> x10, other arithmetic: none -> 8.21 us  [the longest x2 4.32 us: sigma_apply(): stacked = jnp.concatenate(gathered, axis=0)]
  transfers between devices with their start and end apart: 12 -> 20, of which waited for: 12 -> 20; matrix products, arithmetic and copies ran while one was open for 7% -> 8% of each run, Pallas kernels for 0% -> 0%
where the time goes in v1:
time: 647 us; the launch traced here: 637 us
  waiting for transfers between devices  326 us (50%)
  blocking collectives  137 us (21%)
  matrix products  94.3 us (15%)
  between operations  31 us (5%)
  other arithmetic  19.6 us (3%)
  local copies, waits for them, and re-layouts  15.5 us (2%)
  starting transfers between devices  13.2 us (2%)
    reduce_scatter x2, waiting for transfers between devices, sigma_apply(): lax.psum_scatter(combined[None], 'pair', scatter_dimension=1, tiled=True)  137 us
    dot_general x24, matrix products, product(): jnp.dot(first, second, precision=highest, preferred_element_type=jnp.floa...  94.3 us
    all_gather x2, waiting for transfers between devices, sigma_apply(): lax.all_gather(upper_rows, 'pair', axis=1, tiled=True)  77.8 us
    ppermute x8, waiting for transfers between devices, process_packet(): ppermute(w2, axis_name=row_axis, perm=[(hop_no, hop_no ^ y) for hop_no in...  60.2 us
    psum x1, blocking collectives, per_device(): lax.psum((jnp.sum(wavefunction * wavefunction), jnp.sum(wavefunction * fi...  49.3 us
    psum x1, blocking collectives, per_device(): lax.psum((jnp.sum(basis * second_image), jnp.sum(vector * second_image)),...  49.2 us
    all_gather x2, waiting for transfers between devices, sigma_apply(): lax.all_gather(vector, 'pair', axis=1, tiled=True)  43.9 us
    psum x1, blocking collectives, per_device(): lax.psum((jnp.sum(vector * correction), jnp.sum(correction * correction))...  38.5 us
  transfers between devices with their start and end apart: 20, of which 20 were waited for; matrix products, arithmetic and copies ran while one was open for 8% of the time, Pallas kernels for 0%

profile of v1, /device:TPU:12, one launch (start us, length us, event | category | flops | bytes accessed | tf_op | source)
XLA Modules:
  0.0 637.0 jit_solution(17018722894604995330)
XLA Ops:
  14.4 4.5 collective-permute-done.2
  19.5 6.3 collective-permute-done.3
  40.2 11.7 %collective-permute-done.4 = f32[8,1,32,512]{3,2,1,0:T(8,128)} collective-permute-done((f32[8,1,32,512]{3,2,1,0:T(8,128)}, f32[8,1,32,512]{3,2,1,0:T(8,128)}, u32[]{:S(2)}, u32[]{:S(2)}) %collective-permute-start.4) | collective-permute-done | bytes 524320 | tf_op jit(solution)/shard_map/ppermute | solution.py:24
  54.2 25.0 %all-gather.5.cloned.1.call-done = f32[1,512,512]{2,1,0:T(8,128)} async-done(((f32[1,32,512]{2,1,0:T(8,128)}), f32[1,512,512]{2,1,0:T(8,128)}) %all-gather.5.cloned.1.call-update) | async-done | bytes 1048592 | tf_op jit(solution)/shard_map/all_gather | solution.py:58
  79.2 3.1 fusion.82
  84.3 4.0 fusion.21
  88.4 2.9 fusion.72
  94.1 42.4 %all-gather.7.cloned.1.call-done = f32[1,512,512]{2,1,0:T(8,128)} async-done(((f32[1,32,512]{2,1,0:T(8,128)}), f32[1,512,512]{2,1,0:T(8,128)}) %all-gather.7.cloned.1.call-update) | async-done | bytes 1048592 | tf_op jit(solution)/shard_map/all_gather | solution.py:59
  142.8 4.1 fusion.23
  148.2 2.9 fusion.18
  151.1 4.2 fusion.25
  156.5 2.9 fusion.14
  165.3 14.5 %fusion.39 = f32[1,512,512]{2,1,0:T(8,128)} fusion(f32[512,512]{1,0:T(8,128)S(1)} %collective-permute-done.6, f32[512,512]{1,0:T(8,128)S(1)} %collective-permute-done.5, f32[512,512]{1,0:T(8,128)S(1)} %fusion.52, f32[3,512,512]{2,1,0:T(8,128)} %fusion.14, f32[3,1,512,512]{3,2,1,0:T(8,128)S(1)} %copy-done.1, f32[]{:T(128)} %bitcast.20), kind=kOutput, calls=%fused_computation.53 | convolution fusion | flops 1611661312 | bytes 6291460 | tf_op jit(solution)/shard_map/dot_general | solution.py:50
  179.9 68.7 %reduce-scatter.3.cloned.1.call-done = f32[1,32,512]{2,1,0:T(8,128)} async-done(((f32[1,512,512]{2,1,0:T(8,128)}), f32[1,32,512]{2,1,0:T(8,128)}) %reduce-scatter.3.cloned.1.call-update) | async-done | bytes 65552 | tf_op jit(solution)/shard_map/reduce_scatter | solution.py:82
  250.0 49.3 %all-reduce.2 = (f32[]{:T(128)}, f32[]{:T(128)}) all-reduce(f32[]{:T(128)} %get-tuple-element.80, f32[]{:T(128)} %get-tuple-element.79), channel_id=1, replica_groups=mesh['pair'=16,'sector'=2] {'pair','sector'}, use_global_device_ids=true, to_apply=%region_4.5 | all-reduce | flops 2 | bytes 16 | tf_op jit(solution)/shard_map/psum | solution.py:87
  302.9 38.5 %all-reduce.1 = (f32[]{:T(128)}, f32[]{:T(128)}) all-reduce(f32[]{:T(128)} %get-tuple-element.78, f32[]{:T(128)} %get-tuple-element.77), channel_id=1, replica_groups=mesh['pair'=16,'sector'=2] {'pair','sector'}, use_global_device_ids=true, to_apply=%region_8.9 | all-reduce | flops 2 | bytes 16 | tf_op jit(solution)/shard_map/psum | solution.py:97
  350.6 5.0 collective-permute-done.9
  358.2 5.0 collective-permute-done.10
  366.8 22.6 %collective-permute-done.11 = f32[8,1,32,512]{3,2,1,0:T(8,128)} collective-permute-done((f32[8,1,32,512]{3,2,1,0:T(8,128)}, f32[8,1,32,512]{3,2,1,0:T(8,128)}, u32[]{:S(2)}, u32[]{:S(2)}) %collective-permute-start.11) | collective-permute-done | bytes 524320 | tf_op jit(solution)/shard_map/ppermute | solution.py:24
  391.7 18.8 %all-gather.9.cloned.1.call-done = f32[1,512,512]{2,1,0:T(8,128)} async-done(((f32[1,32,512]{2,1,0:T(8,128)}), f32[1,512,512]{2,1,0:T(8,128)}) %all-gather.9.cloned.1.call-update) | async-done | bytes 1048592 | tf_op jit(solution)/shard_map/all_gather | solution.py:58
  410.6 4.7 fusion.50
  417.3 5.7 fusion.10
  423.0 4.5 fusion.48
  427.5 4.7 fusion.46
  432.2 35.5 %all-gather.11.cloned.1.call-done = f32[1,512,512]{2,1,0:T(8,128)} async-done(((f32[1,32,512]{2,1,0:T(8,128)}), f32[1,512,512]{2,1,0:T(8,128)}) %all-gather.11.cloned.1.call-update) | async-done | bytes 1048592 | tf_op jit(solution)/shard_map/all_gather | solution.py:59
  473.7 4.2 fusion.29
  479.2 4.5 fusion.7
  483.7 4.4 fusion.31
  489.4 4.5 fusion.3
  499.9 4.3 fusion.36
  504.2 68.7 %reduce-scatter.5.cloned.1.call-done = f32[1,32,512]{2,1,0:T(8,128)} async-done(((f32[1,512,512]{2,1,0:T(8,128)}), f32[1,32,512]{2,1,0:T(8,128)}) %reduce-scatter.5.cloned.1.call-update) | async-done | bytes 65552 | tf_op jit(solution)/shard_map/reduce_scatter | solution.py:82
  574.3 49.2 %all-reduce = (f32[]{:T(128)}, f32[]{:T(128)}) all-reduce(f32[]{:T(128)} %get-tuple-element.76, f32[]{:T(128)} %get-tuple-element.75), channel_id=1, replica_groups=mesh['pair'=16,'sector'=2] {'pair','sector'}, use_global_device_ids=true, to_apply=%region_13.14 | all-reduce | flops 2 | bytes 16 | tf_op jit(solution)/shard_map/psum | solution.py:104
  (115 shorter events, 75.0 us)
Async XLA Ops:
  7.2 24.0 %copy-start.18 = (s32[3]{0:T(128)S(1)}, s32[3]{0:T(128)}, u32[]{:S(2)}) copy-start(s32[3]{0:T(128)} %param.22) | copy-start | bytes 40
  7.2 30.4 %copy-start.19 = (s32[1,3]{1,0:T(1,128)S(1)}, s32[1,3]{1,0:T(1,128)}, u32[]{:S(2)}) copy-start(s32[1,3]{1,0:T(1,128)} %param.23) | copy-start | bytes 40
  7.2 72.0 %all-gather.5.cloned.1.call-start = ((), (), s32[]{:S(2)}) async-start(), calls=%async_computation.2 | async-start | bytes 1114112 | tf_op jit(solution)/shard_map/all_gather | solution.py:58
  7.9 128.6 %all-gather.7.cloned.1.call-start = ((), (), s32[]{:S(2)}) async-start(), calls=%async_computation.3 | async-start | bytes 1114112 | tf_op jit(solution)/shard_map/all_gather | solution.py:59
  8.0 1.5 collective-permute-start
  9.5 4.3 collective-permute-start.1
  13.8 5.0 collective-permute-start.2
  18.9 6.9 %collective-permute-start.3 = (f32[4,1,32,512]{3,2,1,0:T(8,128)S(1)}, f32[4,1,32,512]{3,2,1,0:T(8,128)}, u32[]{:S(2)}, u32[]{:S(2)}) collective-permute-start(f32[4,1,32,512]{3,2,1,0:T(8,128)S(1)} %pad_maximum_fusion.6), channel_id=1, source_target_pairs={{0,8},{2,10},{4,12},{6,14},{8,0},{10,2},{12,4},{14,6},{16,24},{18,... | collective-permute-start | bytes 786440 | tf_op jit(solution)/shard_map/ppermute | solution.py:24
  19.5 59.7 %copy-start = (f32[3,1,512,512]{3,2,1,0:T(8,128)S(1)}, f32[3,1,512,512]{3,2,1,0:T(8,128)}, u32[]{:S(2)}) copy-start(f32[3,1,512,512]{3,2,1,0:T(8,128)} %param.20) | copy-start | bytes 9437188
  28.4 23.5 %collective-permute-start.4 = (f32[8,1,32,512]{3,2,1,0:T(8,128)}, f32[8,1,32,512]{3,2,1,0:T(8,128)}, u32[]{:S(2)}, u32[]{:S(2)}) collective-permute-start(f32[8,1,32,512]{3,2,1,0:T(8,128)} %pad_maximum_fusion.4), channel_id=1, source_target_pairs={{0,16},{2,18},{4,20},{6,22},{8,24},{10,26},{12,28},{14,30},{16,0},... | collective-permute-start | bytes 1572872 | tf_op jit(solution)/shard_map/ppermute | solution.py:24
  31.1 217.5 %reduce-scatter.3.cloned.1.call-start = ((), (), s32[]{:S(2)}) async-start(), calls=%async_computation.4 | async-start | bytes 1114112 | tf_op jit(solution)/shard_map/reduce_scatter | solution.py:82
  82.3 6.1 copy-start.3
  142.5 5.7 copy-start.8
  161.1 2.7 collective-permute-start.5
  161.2 4.1 collective-permute-start.6
  163.6 85.0 %copy-start.9 = (f32[1,32,512]{2,1,0:T(8,128)S(1)}, f32[1,32,512]{2,1,0:T(8,128)}, u32[]{:S(2)}) copy-start(f32[1,32,512]{2,1,0:T(8,128)} %param.18) | copy-start | bytes 196612
  163.6 137.8 %copy-start.17 = (f32[1,32,512]{2,1,0:T(8,128)S(1)}, f32[1,32,512]{2,1,0:T(8,128)}, u32[]{:S(2)}) copy-start(f32[1,32,512]{2,1,0:T(8,128)} %param.19) | copy-start | bytes 196612
  179.8 230.7 %all-gather.9.cloned.1.call-start = ((), (), s32[]{:S(2)}) async-start(), calls=%async_computation.5 | async-start | bytes 1114112 | tf_op jit(solution)/shard_map/all_gather | solution.py:58
  344.6 123.1 %all-gather.11.cloned.1.call-start = ((), (), s32[]{:S(2)}) async-start(), calls=%async_computation.6 | async-start | bytes 1114112 | tf_op jit(solution)/shard_map/all_gather | solution.py:59
  344.7 1.5 collective-permute-start.7
  346.2 20.5 %copy-start.16 = (f32[1,32,512]{2,1,0:T(8,128)}, f32[1,32,512]{2,1,0:T(8,128)S(1)}, u32[]{:S(2)}) copy-start(f32[1,32,512]{2,1,0:T(8,128)S(1)} %collective-permute-done.7) | copy-start | bytes 196612
  346.2 4.3 collective-permute-start.8
  350.5 5.0 collective-permute-start.9
  355.6 7.6 %collective-permute-start.10 = (f32[4,1,32,512]{3,2,1,0:T(8,128)S(1)}, f32[4,1,32,512]{3,2,1,0:T(8,128)S(1)}, u32[]{:S(2)}, u32[]{:S(2)}) collective-permute-start(f32[4,1,32,512]{3,2,1,0:T(8,128)S(1)} %pad_maximum_fusion.7), channel_id=1, source_target_pairs={{0,8},{2,10},{4,12},{6,14},{8,0},{10,2},{12,4},{14,6},{16,24},{18,... | collective-permute-start | bytes 786440 | tf_op jit(solution)/shard_map/ppermute | solution.py:24
  364.8 24.6 %collective-permute-start.11 = (f32[8,1,32,512]{3,2,1,0:T(8,128)}, f32[8,1,32,512]{3,2,1,0:T(8,128)}, u32[]{:S(2)}, u32[]{:S(2)}) collective-permute-start(f32[8,1,32,512]{3,2,1,0:T(8,128)} %pad_maximum_fusion.5), channel_id=1, source_target_pairs={{0,16},{2,18},{4,20},{6,22},{8,24},{10,26},{12,28},{14,30},{16,0},... | collective-permute-start | bytes 1572872 | tf_op jit(solution)/shard_map/ppermute | solution.py:24
  366.8 206.1 %reduce-scatter.5.cloned.1.call-start = ((), (), s32[]{:S(2)}) async-start(), calls=%async_computation.7 | async-start | bytes 1114112 | tf_op jit(solution)/shard_map/reduce_scatter | solution.py:82
  415.3 7.7 %copy-start.4 = (f32[1,512,512]{2,1,0:T(8,128)S(1)}, f32[1,512,512]{2,1,0:T(8,128)}, u32[]{:S(2)}) copy-start(f32[1,512,512]{2,1,0:T(8,128)} %all-gather.9.cloned.1.call-done) | copy-start | bytes 3145732
  483.7 5.7 copy-start.5
  495.6 2.7 collective-permute-start.12
  495.7 4.1 collective-permute-start.13
  498.1 74.7 %copy-start.13 = (f32[1,32,512]{2,1,0:T(8,128)S(1)}, f32[1,32,512]{2,1,0:T(8,128)}, u32[]{:S(2)}) copy-start(f32[1,32,512]{2,1,0:T(8,128)} %subtract_multiply_fusion) | copy-start | bytes 196612
  498.2 130.0 %copy-start.14 = (f32[1,32,512]{2,1,0:T(8,128)S(1)}, f32[1,32,512]{2,1,0:T(8,128)}, u32[]{:S(2)}) copy-start(f32[1,32,512]{2,1,0:T(8,128)} %reduce-scatter.3.cloned.1.call-done) | copy-start | bytes 196612
  (8 other events, 25.6 us)
Sparse Core Ops, SparseCore 0:
  10.7 68.3 all-gather.4
  82.5 53.9 all-gather.6
  180.0 68.5 reduce-scatter.2
  344.8 65.7 all-gather.8
  413.7 53.9 all-gather.10
  504.3 68.5 reduce-scatter.4
